TPU v7x, 32 devices: a whole 2x2x4 slice. The times are simulated.
32 devices in a mesh: dp: 32 (over z, y, x, core).
Axes of the slice: x: 2, y: 2, z: 4, core: 2. Of those that a mesh axis runs over, the one named last changes fastest.
Arguments:
- hidden: bfloat16 [32768, 5120], P('dp'), may hold values from -6 to 6
- norm_gain: float32 [5120], replicated, may hold values from 0.25 to 4
- q_cotangent: bfloat16 [32768, 128], P('dp'), may hold values from -0.03125 to 0.03125
- head_output: bfloat16 [32768, 128], P('dp'), may hold values from -6 to 6
- out_cotangent: bfloat16 [32768, 5120], P('dp'), may hold values from -0.0625 to 0.0625
- master_q: float32 [5120, 128], P('dp'), may hold values from -0.125 to 0.125
- moment_q: float32 [5120, 128], P('dp'), may hold values from -6 to 6
- second_q: float32 [5120, 128], P('dp'), may hold values from 0.01 to 0.5
- master_o: float32 [128, 5120], P(None, 'dp'), may hold values from -0.0234375 to 0.0234375
- moment_o: float32 [128, 5120], P(None, 'dp'), may hold values from -6 to 6
- second_o: float32 [128, 5120], P(None, 'dp'), may hold values from 0.01 to 0.5
Outputs:
- q_param: bfloat16 [5120, 128], replicated
- o_param: bfloat16 [128, 5120], replicated
- master_q_new: float32 [5120, 128], P('dp')
- moment_q_new: float32 [5120, 128], P('dp')
- second_q_new: float32 [5120, 128], P('dp')
- master_o_new: float32 [128, 5120], P(None, 'dp')
- moment_o_new: float32 [128, 5120], P(None, 'dp')
- second_o_new: float32 [128, 5120], P(None, 'dp')
- grad_rms: float32 [], replicated
All inputs are finite; a program needn't handle non-finite values.
Results may differ from a plain program's by a relative error of at most 0.0026.
Values may be sent and summed in bfloat16 or wider, within the bound.
A program may use at most 128 MiB of HBM per device.

v0:
```python
import jax
import jax.numpy as jnp
from jax import lax
from jax.sharding import PartitionSpec as P

D = 5120
WIDTH = 128
STEP = 20


norm_eps = 1e-05
beta_one = 0.9
beta_two = 0.95
learn_rate = 0.001
decay_rate = 0.1
adam_eps = 1e-08
clip_rms = 1.0


def normalize(hidden_block, norm_gain):
    hidden_wide = hidden_block.astype(jnp.float32)
    inverse = lax.rsqrt(jnp.mean(hidden_wide * hidden_wide, axis=1, keepdims=True) + norm_eps)
    return (hidden_wide * inverse * norm_gain[None, :]).astype(jnp.bfloat16)


def adamw(master, moment, second, gradient, factor):
    clipped = gradient * factor
    moment_new = beta_one * moment + (1.0 - beta_one) * clipped
    second_new = beta_two * second + (1.0 - beta_two) * clipped * clipped
    first_fix = 1.0 - beta_one**STEP
    second_fix = 1.0 - beta_two**STEP
    update = moment_new / first_fix / (jnp.sqrt(second_new / second_fix) + adam_eps)
    master_new = master - learn_rate * (update + decay_rate * master)
    return (master_new, moment_new, second_new)


def shards(
    hidden,
    norm_gain,
    q_cotangent,
    head_output,
    out_cotangent,
    master_q,
    moment_q,
    second_q,
    master_o,
    moment_o,
    second_o,
):
    normed = normalize(hidden, norm_gain)
    joined = lax.psum_scatter(
        jnp.concatenate(
            [
                jnp.dot(normed.T, q_cotangent, preferred_element_type=jnp.float32),
                jnp.dot(out_cotangent.T, head_output, preferred_element_type=jnp.float32),
            ],
            axis=1,
        ),
        "dp",
        scatter_dimension=0,
        tiled=True,
    )
    grad_query = joined[:, :WIDTH]
    grad_turned = joined[:, WIDTH:]
    grad_outer = grad_turned.T
    local_square = jnp.sum(grad_query * grad_query) + jnp.sum(grad_outer * grad_outer)
    total_square = lax.psum(local_square, "dp")
    grad_rms = jnp.sqrt(total_square / (2.0 * D * WIDTH))
    factor = jnp.minimum(1.0, clip_rms / grad_rms)
    master_q_new, moment_q_new, second_q_new = adamw(
        master_q, moment_q, second_q, grad_query, factor
    )
    master_o_new, moment_o_new, second_o_new = adamw(
        master_o, moment_o, second_o, grad_outer, factor
    )
    query_half = master_q_new.astype(jnp.bfloat16)
    outer_half = master_o_new.astype(jnp.bfloat16)
    q_param, outer_turned = (
        lax.all_gather(query_half, "dp", axis=0, tiled=True),
        lax.all_gather(outer_half.T, "dp", axis=0, tiled=True),
    )
    o_param = outer_turned.T
    return (
        q_param,
        o_param,
        master_q_new,
        moment_q_new,
        second_q_new,
        master_o_new,
        moment_o_new,
        second_o_new,
        grad_rms,
    )


def solution(mesh):
    in_specs = (
        P("dp", None),
        P(),
        P("dp", None),
        P("dp", None),
        P("dp", None),
        P("dp", None),
        P("dp", None),
        P("dp", None),
        P(None, "dp"),
        P(None, "dp"),
        P(None, "dp"),
    )
    out_specs = (
        P(),
        P(),
        P("dp", None),
        P("dp", None),
        P("dp", None),
        P(None, "dp"),
        P(None, "dp"),
        P(None, "dp"),
        P(),
    )
    return jax.shard_map(shards, mesh=mesh, in_specs=in_specs, out_specs=out_specs, check_vma=False)
```

profile of v0, /device:TPU:1, one launch (start us, length us, event | category | flops | bytes accessed | tf_op | source)
XLA Modules:
  0.0 340.8 jit_solution(9492823869190335668)
XLA Ops:
  7.2 0.0 copy-start
  7.2 0.0 reduce-scatter.4.cloned.1.call-start
  7.2 0.0 copy-start.1
  7.2 0.0 copy-start.9
  7.3 0.0 copy-start.10
  7.3 6.2 %fusion = f32[1024]{0:T(1024)S(1)} fusion(bf16[1024,5120]{1,0:T(8,128)(2,1)} %param.11), kind=kLoop, calls=%fused_computation.2 | loop fusion | flops 15727616 | bytes 10489856 | tf_op jit(solution)/shard_map/reduce_sum | solution.py:22
  13.5 0.0 copy-done
  13.5 0.7 copy-done.1
  14.2 1.6 fusion.14
  15.9 2.1 copy-done.2
  18.0 3.4 fusion.3
  21.4 2.7 pad_maximum_fusion
  24.1 0.0 copy-start.7
  24.1 0.0 copy-start.8
  24.1 6.0 %copy.55 = f32[5120,256]{1,0:T(8,128)} copy(f32[5120,256]{0,1:T(8,128)} %pad_maximum_fusion) | data formatting | bytes 10485760
  30.1 0.0 reduce-scatter.4.cloned.1.call-update
  30.1 0.0 all-gather.5.cloned.1.call-start
  30.2 141.0 %reduce-scatter.4.cloned.1.call-done = f32[160,256]{1,0:T(8,128)} async-done(((f32[5120,256]{1,0:T(8,128)}), f32[160,256]{1,0:T(8,128)}) %reduce-scatter.4.cloned.1.call-update) | async-done | bytes 163856 | tf_op jit(solution)/shard_map/reduce_scatter | solution.py:51
  171.2 1.6 multiply_reduce_fusion
  174.0 41.6 %psum.7 = f32[]{:T(128)} all-reduce(f32[]{:T(128)S(6)} %add.50), channel_id=1, replica_groups=mesh['dp'=32] {'dp'}, use_global_device_ids=true, to_apply=%region_4.0 | all-reduce | flops 1 | bytes 8 | tf_op jit(solution)/shard_map/psum | solution.py:67
  216.4 1.6 convert_bitcast_fusion
  218.0 0.0 all-gather.5.cloned.1.call-update
  218.1 0.0 all-gather.3.cloned.1.call-start
  218.1 0.0 copy-done.6
  218.1 0.0 copy-done.7
  218.1 0.0 copy-done.8
  218.1 1.6 fusion.12
  219.8 0.0 all-gather.3.cloned.1.call-update
  219.8 54.3 %all-gather.5.cloned.1.call-done = bf16[5120,128]{1,0:T(8,128)(2,1)} async-done(((bf16[160,128]{1,0:T(8,128)(2,1)}), bf16[5120,128]{1,0:T(8,128)(2,1)}) %all-gather.5.cloned.1.call-update) | async-done | bytes 1310736 | tf_op jit(solution)/shard_map/all_gather | solution.py:80
  274.1 2.4 copy.54
  276.5 54.2 %all-gather.3.cloned.1.call-done = bf16[5120,128]{1,0:T(8,128)(2,1)} async-done(((bf16[160,128]{1,0:T(8,128)(2,1)}), bf16[5120,128]{1,0:T(8,128)(2,1)}) %all-gather.3.cloned.1.call-update) | async-done | bytes 1310736 | tf_op jit(solution)/shard_map/all_gather | solution.py:79
  330.7 2.5 copy.58
  (11 shorter events, 0.0 us)
Async XLA Ops:
  7.2 6.3 %copy-start = (bf16[1024,128]{1,0:T(8,128)(2,1)S(1)}, bf16[1024,128]{1,0:T(8,128)(2,1)}, u32[]{:S(2)}) copy-start(bf16[1024,128]{1,0:T(8,128)(2,1)} %param.14) | copy-start | bytes 786436
  7.2 164.0 %reduce-scatter.4.cloned.1.call-start = ((), (), s32[]{:S(2)}) async-start(), calls=%async_computation.3 | async-start | bytes 5406720 | tf_op jit(solution)/shard_map/reduce_scatter | solution.py:51
  7.2 7.0 %copy-start.1 = (bf16[1024,5120]{1,0:T(8,128)(2,1)S(1)}, bf16[1024,5120]{1,0:T(8,128)(2,1)}, u32[]{:S(2)}) copy-start(bf16[1024,5120]{1,0:T(8,128)(2,1)} %param.15) | copy-start | bytes 31457284
  7.2 8.6 %copy-start.9 = (bf16[1024,128]{1,0:T(8,128)(2,1)S(1)}, bf16[1024,128]{1,0:T(8,128)(2,1)}, u32[]{:S(2)}) copy-start(bf16[1024,128]{1,0:T(8,128)(2,1)} %param.13) | copy-start | bytes 786436
  7.3 8.6 %copy-start.10 = (f32[5120]{0:T(1024)S(1)}, f32[5120]{0:T(1024)}, u32[]{:S(2)}) copy-start(f32[5120]{0:T(1024)} %param.12) | copy-start | bytes 61444
  13.5 4.5 %copy-start.2 = (bf16[1024,5120]{1,0:T(8,128)(2,1)S(1)}, bf16[1024,5120]{1,0:T(8,128)(2,1)}, u32[]{:S(2)}) copy-start(bf16[1024,5120]{1,0:T(8,128)(2,1)} %param.11) | copy-start | bytes 31457284
  24.1 192.3 %copy-start.3 = (f32[128,160]{0,1:T(8,128)S(1)}, f32[128,160]{0,1:T(8,128)}, u32[]{:S(2)}) copy-start(f32[128,160]{0,1:T(8,128)} %param.19) | copy-start | bytes 245764
  24.1 192.3 %copy-start.4 = (f32[128,160]{0,1:T(8,128)S(1)}, f32[128,160]{0,1:T(8,128)}, u32[]{:S(2)}) copy-start(f32[128,160]{0,1:T(8,128)} %param.20) | copy-start | bytes 245764
  24.1 192.3 %copy-start.5 = (f32[128,160]{0,1:T(8,128)S(1)}, f32[128,160]{0,1:T(8,128)}, u32[]{:S(2)}) copy-start(f32[128,160]{0,1:T(8,128)} %param.21) | copy-start | bytes 245764
  24.1 194.0 %copy-start.6 = (f32[160,128]{1,0:T(8,128)S(1)}, f32[160,128]{1,0:T(8,128)}, u32[]{:S(2)}) copy-start(f32[160,128]{1,0:T(8,128)} %param.16) | copy-start | bytes 245764
  24.1 194.0 %copy-start.7 = (f32[160,128]{1,0:T(8,128)S(1)}, f32[160,128]{1,0:T(8,128)}, u32[]{:S(2)}) copy-start(f32[160,128]{1,0:T(8,128)} %param.17) | copy-start | bytes 245764
  24.1 194.0 %copy-start.8 = (f32[160,128]{1,0:T(8,128)S(1)}, f32[160,128]{1,0:T(8,128)}, u32[]{:S(2)}) copy-start(f32[160,128]{1,0:T(8,128)} %param.18) | copy-start | bytes 245764
  30.1 244.0 %all-gather.5.cloned.1.call-start = ((), (), s32[]{:S(2)}) async-start(), calls=%async_computation.2 | async-start | bytes 1351680 | tf_op jit(solution)/shard_map/all_gather | solution.py:80
  218.1 112.6 %all-gather.3.cloned.1.call-start = ((), (), s32[]{:S(2)}) async-start(), calls=%async_computation.1 | async-start | bytes 1351680 | tf_op jit(solution)/shard_map/all_gather | solution.py:79
Sparse Core Ops, SparseCore 0:
  30.2 140.9 reduce-scatter.3
  218.2 55.8 all-gather.4
  277.5 53.1 all-gather.2
where the time goes:
time: 342 us; the launch traced here: 341 us
  waiting for transfers between devices  250 us (73%)
  blocking collectives  41.6 us (12%)
  between operations  17.1 us (5%)
  local copies, waits for them, and re-layouts  13.7 us (4%)
  other arithmetic  13.7 us (4%)
  matrix products  5.05 us (1%)
    reduce_scatter x1, waiting for transfers between devices, shards(): lax.psum_scatter(jnp.concatenate([jnp.dot(normed.T, q_cotangent, preferre...  141 us
    all_gather x1, waiting for transfers between devices, shards(): lax.all_gather(outer_half.T, 'dp', axis=0, tiled=True)  54.3 us
    all_gather x1, waiting for transfers between devices, shards(): lax.all_gather(query_half, 'dp', axis=0, tiled=True)  54.2 us
    psum x1, blocking collectives, shards(): total_square = lax.psum(local_square, 'dp')  41.6 us
    unnamed x25, local copies, waits for them, and re-layouts  13.7 us
  transfers between devices with their start and end apart: 3, of which 3 were waited for; matrix products, arithmetic and copies ran while one was open for 1% of the time, Pallas kernels for 0%

commit v1 on v0

v1 whole, which is shorter than its diff:
```python
import functools
import math

import jax
import jax.numpy as jnp
from jax import lax
from jax.experimental import pallas as pl
from jax.experimental.pallas import tpu as pltpu
from jax.sharding import PartitionSpec as P

STEP = 20
norm_eps = 1e-05
beta_one = 0.9
beta_two = 0.95
learn_rate = 0.001
decay_rate = 0.1
adam_eps = 1e-08
clip_rms = 1.0
MESH = pl.DeviceIdType.MESH
F32 = jnp.float32
BF16 = jnp.bfloat16


def adamw(master, moment, second, gradient, factor):
    clipped = gradient * factor
    moment_new = beta_one * moment + (1.0 - beta_one) * clipped
    second_new = beta_two * second + (1.0 - beta_two) * clipped * clipped
    first_fix = 1.0 - beta_one**STEP
    second_fix = 1.0 - beta_two**STEP
    update = moment_new / first_fix / (jnp.sqrt(second_new / second_fix) + adam_eps)
    master_new = master - learn_rate * (update + decay_rate * master)
    return (master_new, moment_new, second_new)


def kernel(
    n, s, zs,
    hid_ref, gain_ref, qt_ref, ht_ref, oc_ref, st_ref,
    gbuf, new_ref, rms_ref,
    hid, oc, inv, part, crecv, asend, arecv, bsend, brecv, zsend, zrecv, sbuf,
    hsem, osem, c_s, c_r, a_s, a_r, b_s, b_r, z_s, z_r, s_s, s_r,
    gz_s, gz_r, gb_s, gb_r, ga_s, ga_r, gc_s, gc_r,
):
    tokens, width = hid.shape
    rows = part.shape[2]
    me = lax.axis_index("dp")
    core = me % 2
    x = (me // 2) % s
    y = (me // (2 * s)) % s
    z = me // (2 * s * s)
    a = x + core * (y - x)
    b = y + core * (x - y)
    other = 1 - core

    def dev(c, a_at, b_at, z_at):
        x_at = a_at + c * (b_at - a_at)
        y_at = b_at + c * (a_at - b_at)
        return ((z_at * s + y_at) * s + x_at) * 2 + c

    def remote(src, dst, ss, rs, to):
        return pltpu.make_async_remote_copy(
            src_ref=src, dst_ref=dst, send_sem=ss, recv_sem=rs, device_id=(to,), device_id_type=MESH
        )

    chunk = rows * 128 // math.gcd(rows, 128)
    chunk = chunk * max(1, 640 // chunk)
    steps = width // chunk
    per = chunk // rows
    hrow = tokens // 4

    oc_in = [
        pltpu.make_async_copy(oc_ref.at[:, pl.ds(i * chunk, chunk)], oc.at[:, pl.ds(i * chunk, chunk)], osem.at[i])
        for i in range(steps)
    ]
    hid_in = [
        pltpu.make_async_copy(hid_ref.at[pl.ds(i * hrow, hrow)], hid.at[pl.ds(i * hrow, hrow)], hsem.at[i])
        for i in range(4)
    ]
    for copy in oc_in + hid_in:
        copy.start()

    peer_c = dev(other, b, a, z)
    peer_a = {d: dev(core, (a + d) % s, b, z) for d in range(1, s)}
    peer_b = {d: dev(core, a, (b + d) % s, z) for d in range(1, s)}
    peer_z = {d: dev(core, a, b, (z + d) % zs) for d in range(1, zs)}
    peers = [peer_c] + list(peer_a.values()) + list(peer_b.values()) + list(peer_z.values())
    barrier = pltpu.get_barrier_semaphore()
    for peer in peers:
        pl.semaphore_signal(barrier, inc=1, device_id=(peer,), device_id_type=MESH)
    pl.semaphore_wait(barrier, len(peers))

    sends = []

    def go(copy):
        copy.start()
        sends.append(copy)

    def send_chunk(h, i):
        for k in range(per // 2):
            j = i * per + 2 * k + other
            xj = (j // 2) % s
            yj = (j // (2 * s)) % s
            zj = j // (2 * s * s)
            aj = xj + other * (yj - xj)
            bj = yj + other * (xj - yj)
            d = (aj - b + s) % s
            e = (bj - a + s) % s
            f = (zj - z + zs) % zs
            slot = (d * s + e) * zs + f
            go(remote(part.at[h, j], crecv.at[h, slot], c_s.at[h, slot], c_r.at[h, slot], peer_c))

    def wait_c(h, d, e, f):
        slot = (d * s + e) * zs + f
        remote(part.at[h, 0], crecv.at[h, slot], c_s.at[h, slot], c_r.at[h, slot], peer_c).wait_recv()

    def pair(h, d, e, f):
        j = dev(core, (a + d) % s, (b + e) % s, (z + f) % zs)
        return part[h, j] + crecv[h, (d * s + e) * zs + f]

    e_order = list(range(1, s)) + [0]
    f_order = [f for f in (2, 1, 3) if f < zs] + [0]

    def copy_a(h, d, e, f):
        at = ((d - 1) * s + e) * zs + f
        return remote(asend.at[h, at], arecv.at[h, at], a_s.at[h, at], a_r.at[h, at], peer_a[d])

    def copy_b(h, e, f):
        at = (e - 1) * zs + f
        return remote(bsend.at[h, at], brecv.at[h, at], b_s.at[h, at], b_r.at[h, at], peer_b[e])

    def copy_z(h, f):
        return remote(zsend.at[h, f - 1], zrecv.at[h, f - 1], z_s.at[h, f - 1], z_r.at[h, f - 1], peer_z[f])

    def stage_a(h):
        for e in e_order:
            for f in f_order:
                for d in range(1, s):
                    wait_c(h, d, e, f)
                    asend[h, ((d - 1) * s + e) * zs + f] = pair(h, d, e, f).astype(BF16)
                    go(copy_a(h, d, e, f))

    def after_a(h, e, f):
        wait_c(h, 0, e, f)
        total = pair(h, 0, e, f)
        for d in range(1, s):
            copy_a(h, d, e, f).wait_recv()
            total += arecv[h, ((d - 1) * s + e) * zs + f].astype(F32)
        return total

    def stage_b(h):
        for f in f_order:
            for e in range(1, s):
                bsend[h, (e - 1) * zs + f] = after_a(h, e, f).astype(BF16)
                go(copy_b(h, e, f))

    def after_b(h, f):
        total = after_a(h, 0, f)
        for e in range(1, s):
            copy_b(h, e, f).wait_recv()
            total += brecv[h, (e - 1) * zs + f].astype(F32)
        return total

    def stage_z(h):
        for f in f_order[:-1]:
            zsend[h, f - 1] = after_b(h, f).astype(BF16)
            go(copy_z(h, f))

    def finish(h):
        total = after_b(h, 0)
        for f in range(1, zs):
            copy_z(h, f).wait_recv()
            total += zrecv[h, f - 1].astype(F32)
        return total

    def store(h, i, product):
        turned = product.T
        for k in range(per):
            part[h, i * per + k] = turned[k * rows : (k + 1) * rows]

    head = ht_ref[...]
    for i in range(steps):
        oc_in[i].wait()
        store(0, i, jnp.dot(head, oc[:, i * chunk : (i + 1) * chunk], preferred_element_type=F32))
        send_chunk(0, i)

    group = 16
    for i in range(4):
        hid_in[i].wait()

        @pl.loop(0, hrow // group)
        def squares(t, i=i):
            at = pl.multiple_of(i * hrow + t * group, group)
            wide = hid[pl.ds(at, group)].astype(F32)
            inv[pl.ds(at, group)] = lax.rsqrt(jnp.sum(wide * wide, axis=1, keepdims=True) / width + norm_eps)

    stage_a(0)

    scaled = qt_ref[...].astype(F32) * inv[...]
    high = scaled.astype(BF16)
    low = (scaled - high.astype(F32)).astype(BF16)
    both = jnp.concatenate([high, low], axis=1).T
    cols = qt_ref.shape[1]
    for i in range(steps):
        product = jnp.dot(both, hid[:, i * chunk : (i + 1) * chunk], preferred_element_type=F32)
        store(1, i, (product[:cols] + product[cols:]) * gain_ref[:, i * chunk : (i + 1) * chunk])
        send_chunk(1, i)

    stage_b(0)
    stage_a(1)
    stage_z(0)
    stage_b(1)
    stage_z(1)
    grad_o = finish(0)
    part[0, me] = grad_o
    grad_q = finish(1)
    part[1, me] = grad_q

    square = jnp.sum(grad_q * grad_q) + jnp.sum(grad_o * grad_o)
    value = jnp.full(sbuf.shape[2:], square, F32)
    at_sem = 0
    for stage, (place, size, to) in enumerate(
        ((core, 2, {1: peer_c}), (a, s, peer_a), (b, s, peer_b), (z, zs, peer_z))
    ):
        sbuf[stage, place] = value
        copies = []
        for d in range(1, size):
            copy = remote(sbuf.at[stage, place], sbuf.at[stage, place], s_s.at[at_sem], s_r.at[at_sem], to[d])
            at_sem += 1
            go(copy)
            copies.append((d, copy))
        for d, copy in copies:
            copy.wait_recv()
        value = sbuf[stage, 0]
        for k in range(1, size):
            value = value + sbuf[stage, k]
    rms = jnp.sqrt(value / (2.0 * width * cols))
    rms_ref[...] = rms
    factor = jnp.minimum(1.0, clip_rms / rms)[:1]

    for h in (1, 0):
        master, moment, second = adamw(st_ref[3 * h], st_ref[3 * h + 1], st_ref[3 * h + 2], part[h, me], factor)
        new_ref[3 * h] = master
        new_ref[3 * h + 1] = moment
        new_ref[3 * h + 2] = second
        gbuf[me, h] = master.astype(BF16)

    def shard(d, e, f):
        return gbuf.at[dev(core, (a - d + s) % s, (b - e + s) % s, (z - f + zs) % zs)]

    def gather_z(f):
        return remote(shard(0, 0, 0), shard(0, 0, 0), gz_s.at[f - 1], gz_r.at[f - 1], peer_z[f])

    def gather_b(e, f):
        at = (e - 1) * zs + f
        return remote(shard(0, 0, f), shard(0, 0, f), gb_s.at[at], gb_r.at[at], peer_b[e])

    def gather_a(d, e, f):
        at = ((d - 1) * s + e) * zs + f
        return remote(shard(0, e, f), shard(0, e, f), ga_s.at[at], ga_r.at[at], peer_a[d])

    def gather_c(d, e, f):
        at = (d * s + e) * zs + f
        return remote(shard(d, e, f), shard(d, e, f), gc_s.at[at], gc_r.at[at], peer_c)

    def pass_a(e, f):
        for d in range(1, s):
            go(gather_a(d, e, f))
        go(gather_c(0, e, f))

    def pass_b(f):
        if f:
            gather_z(f).wait_recv()
        for e in range(1, s):
            go(gather_b(e, f))
        pass_a(0, f)

    def from_b(f):
        for e in range(1, s):
            gather_b(e, f).wait_recv()
            pass_a(e, f)

    def from_a(f):
        for e in range(s):
            for d in range(1, s):
                gather_a(d, e, f).wait_recv()
                go(gather_c(d, e, f))

    for f in range(1, zs):
        go(gather_z(f))
    order = [0] + [f for f in (1, 3, 2) if f < zs]
    for t, f in enumerate(order):
        pass_b(f)
        from_b(f)
        if t:
            from_a(order[t - 1])
    from_a(order[-1])
    for d in range(s):
        for e in range(s):
            for f in range(zs):
                gather_c(d, e, f).wait_recv()
    for copy in sends:
        copy.wait_send()


def shards(
    hidden, norm_gain, q_cotangent, head_output, out_cotangent,
    master_q, moment_q, second_q, master_o, moment_o, second_o,
    *, n,
):
    tokens, width = hidden.shape
    rows, cols = master_q.shape
    zs = 4
    s = math.isqrt(n // (2 * zs))
    slots = s * s * zs
    state = jnp.stack([master_o.T, moment_o.T, second_o.T, master_q, moment_q, second_q])
    any_spec = pl.BlockSpec(memory_space=pl.ANY)
    vmem = pl.BlockSpec(memory_space=pltpu.VMEM)
    dma = pltpu.SemaphoreType.DMA
    na, nb, nz = (s - 1) * s * zs, (s - 1) * zs, zs - 1
    tile = (rows, cols)
    gathered, new, rms = pl.pallas_call(
        functools.partial(kernel, n, s, zs),
        out_shape=(
            jax.ShapeDtypeStruct((n, 2) + tile, BF16),
            jax.ShapeDtypeStruct((6,) + tile, F32),
            jax.ShapeDtypeStruct((8, 128), F32),
        ),
        in_specs=[any_spec, vmem, vmem, vmem, any_spec, vmem],
        out_specs=(vmem, vmem, vmem),
        scratch_shapes=[
            pltpu.VMEM((tokens, width), BF16),
            pltpu.VMEM((tokens, width), BF16),
            pltpu.VMEM((tokens, 1), F32),
            pltpu.VMEM((2, n) + tile, F32),
            pltpu.VMEM((2, slots) + tile, F32),
            pltpu.VMEM((2, na) + tile, BF16),
            pltpu.VMEM((2, na) + tile, BF16),
            pltpu.VMEM((2, nb) + tile, BF16),
            pltpu.VMEM((2, nb) + tile, BF16),
            pltpu.VMEM((2, nz) + tile, BF16),
            pltpu.VMEM((2, nz) + tile, BF16),
            pltpu.VMEM((4, max(s, zs), 8, 128), F32),
            dma((4,)), dma((64,)),
            dma((2, slots)), dma((2, slots)),
            dma((2, na)), dma((2, na)),
            dma((2, nb)), dma((2, nb)),
            dma((2, nz)), dma((2, nz)),
            dma((2 * s + zs,)), dma((2 * s + zs,)),
            dma((nz,)), dma((nz,)),
            dma((nb,)), dma((nb,)),
            dma((na,)), dma((na,)),
            dma((slots,)), dma((slots,)),
        ],
        compiler_params=pltpu.CompilerParams(
            collective_id=0, has_side_effects=True, vmem_limit_bytes=60 * 1024 * 1024
        ),
    )(hidden, norm_gain[None, :], q_cotangent, head_output.T, out_cotangent, state)
    q_param = gathered[:, 1].reshape(width, cols)
    o_param = gathered[:, 0].reshape(width, cols).T
    return (
        q_param, o_param,
        new[3], new[4], new[5],
        new[0].T, new[1].T, new[2].T,
        rms[0, 0],
    )


def solution(mesh):
    row, col = P("dp", None), P(None, "dp")
    in_specs = (row, P(), row, row, row, row, row, row, col, col, col)
    out_specs = (P(), P(), row, row, row, col, col, col, P())
    body = functools.partial(shards, n=mesh.shape["dp"])
    return jax.shard_map(body, mesh=mesh, in_specs=in_specs, out_specs=out_specs, check_vma=False)
```

time: 342 us -> 87 us (0.25)
  waiting for transfers between devices: 250 us -> 0 us
  Pallas kernels: 0 us -> 72.4 us
  blocking collectives: 41.6 us -> 0 us
  between operations: 17.1 us -> 0.68 us
  other arithmetic: 13.7 us -> 0 us
  matrix products: 5.05 us -> 0 us
    reduce_scatter x1 -> x0, waiting for transfers between devices: 141 us -> none  [shards(): lax.psum_scatter(jnp.concatenate([jnp.dot(normed.T, q_cotangent, preferre...]
    all_gather x2 -> x0, waiting for transfers between devices: 108 us -> none  [the longest x1 54.3 us: shards(): lax.all_gather(outer_half.T, 'dp', axis=0, tiled=True)]
    pallas_call x0 -> x1, Pallas kernels: none -> 72.4 us  [shards(): pl.pallas_call(functools.partial(kernel, n, s, zs), out_shape=(jax.ShapeD...]
    psum x1 -> x0, blocking collectives: 41.6 us -> none  [shards(): total_square = lax.psum(local_square, 'dp')]
    reduce_sum x2 -> x0, other arithmetic: 7.78 us -> none  [the longest x1 6.23 us: normalize(): jnp.mean(hidden_wide * hidden_wide, axis=1, keepdims=True) + norm_eps]
    unnamed x25 -> x12, local copies, waits for them, and re-layouts: 13.7 us -> 7.07 us
    dot_general x2 -> x0, matrix products: 5.05 us -> none  [the longest x1 3.41 us: shards(): jnp.dot(normed.T, q_cotangent, preferred_element_type=jnp.float32)]
    slice x0 -> x2, local copies, waits for them, and re-layouts: none -> 4.14 us  [the longest x1 2.94 us: shards(): o_param = gathered[:, 0].reshape(width, cols).T]
  transfers between devices with their start and end apart: 3 -> 0, of which waited for: 3 -> 0; matrix products, arithmetic and copies ran while one was open for 1% -> 0% of each run, Pallas kernels for 0% -> 0%
where the time goes in v1:
time: 87 us; the launch traced here: 86.5 us
  Pallas kernels  72.4 us (83%)
  local copies, waits for them, and re-layouts  13.4 us (15%)
    pallas_call x1, Pallas kernels, shards(): pl.pallas_call(functools.partial(kernel, n, s, zs), out_shape=(jax.ShapeD...  72.4 us
    unnamed x12, local copies, waits for them, and re-layouts  7.07 us
    slice x1, local copies, waits for them, and re-layouts, shards(): o_param = gathered[:, 0].reshape(width, cols).T  2.94 us

profile of v1, /device:TPU:1, one launch (start us, length us, event | category | flops | bytes accessed | tf_op | source)
XLA Modules:
  0.0 86.5 jit_solution(11377610960381760419)
XLA Ops:
  0.6 0.0 copy-start.2
  0.7 1.8 %copy.20 = bf16[1024,128]{0,1:T(8,128)(2,1)} copy(bf16[1024,128]{1,0:T(8,128)(2,1)} %param.14) | data formatting | bytes 524288 | tf_op args[3]
  2.5 0.9 %bitcast_dynamic-update-slice_fusion.2 = f32[6,160,128]{2,1,0:T(8,128)S(1)} fusion(f32[128,160]{0,1:T(8,128)} %param.19), kind=kLoop, calls=%fused_computation.2 | loop fusion | bytes 163840
  3.4 0.9 %bitcast_dynamic-update-slice_fusion.1 = f32[6,160,128]{2,1,0:T(8,128)S(1)} fusion(f32[6,160,128]{2,1,0:T(8,128)S(1)} %bitcast_dynamic-update-slice_fusion.2, f32[128,160]{0,1:T(8,128)} %param.20), kind=kLoop, calls=%fused_computation.1 | loop fusion | bytes 163840
  4.3 0.9 %bitcast_dynamic-update-slice_fusion = f32[6,160,128]{2,1,0:T(8,128)S(1)} fusion(f32[6,160,128]{2,1,0:T(8,128)S(1)} %bitcast_dynamic-update-slice_fusion.1, f32[128,160]{0,1:T(8,128)} %param.21), kind=kLoop, calls=%fused_computation | loop fusion | bytes 163840
  5.2 0.9 %bitcast_dynamic-update-slice_fusion.5 = f32[6,160,128]{2,1,0:T(8,128)S(1)} fusion(f32[6,160,128]{2,1,0:T(8,128)S(1)} %bitcast_dynamic-update-slice_fusion, f32[160,128]{1,0:T(8,128)} %param.16), kind=kLoop, calls=%fused_computation.5 | loop fusion | bytes 163840
  6.0 0.9 %bitcast_dynamic-update-slice_fusion.4 = f32[6,160,128]{2,1,0:T(8,128)S(1)} fusion(f32[6,160,128]{2,1,0:T(8,128)S(1)} %bitcast_dynamic-update-slice_fusion.5, f32[160,128]{1,0:T(8,128)} %param.17), kind=kLoop, calls=%fused_computation.4 | loop fusion | bytes 163840
  6.9 0.0 copy-done.2
  7.0 0.0 copy-start
  7.0 0.8 copy-done
  7.7 72.4 %shard_map.178 = (bf16[32,2,160,128]{3,2,1,0:T(8,128)(2,1)}, f32[6,160,128]{2,1,0:T(8,128)}, f32[8,128]{1,0:T(8,128)}) custom-call(bf16[1024,5120]{1,0:T(8,128)(2,1)} %hid_ref.1, f32[1,5120]{1,0:T(1,128)} %bitcast.46, bf16[1024,128]{1,0:T(8,128)(2,1)} %qt_ref.1, bf16[128,1024]{1,0:T(8,128)(2,1)} %bitcast.45, bf16[1024,5120]{1,0:T(8,128)(2,1)} %oc_ref.1, ...), custom_call_target="tpu_custom_call" | custom-call | tf_op jit(solution)/shard_map/pallas_call | solution.py:320
  80.2 1.2 %slice.35 = f32[1,1]{1,0:T(1,128)} slice(f32[8,128]{1,0:T(8,128)} %get-tuple-element.14), slice={[0:1], [0:1]} | slice | bytes 8 | tf_op jit(solution)/shard_map/slice | solution.py:363
  81.4 2.9 %fusion = (bf16[32,1,160,128]{3,2,1,0:T(8,128)(2,1)S(1)}, bf16[32,1,160,128]{3,2,1,0:T(8,128)(2,1)}) fusion(bf16[32,2,160,128]{3,2,1,0:T(8,128)(2,1)} %get-tuple-element.12), kind=kLoop, calls=%fused_computation.12 | loop fusion | bytes 5242880 | tf_op jit(solution)/shard_map/slice | solution.py:358
  84.3 0.0 copy-start.1
  84.3 1.4 %copy.21 = bf16[5120,128]{0,1:T(8,128)(2,1)} copy(bf16[5120,128]{1,0:T(8,128)(2,1)S(1)} %bitcast.42) | data formatting | bytes 2621440 | tf_op jit(solution)/shard_map/reshape;squeeze | solution.py:358
  85.8 0.0 copy-done.1
  85.8 0.8 slice_bitcast_fusion
  (1 shorter events, 0.0 us)
Async XLA Ops:
  0.6 6.3 %copy-start.2 = (f32[160,128]{1,0:T(8,128)S(1)}, f32[160,128]{1,0:T(8,128)}, u32[]{:S(2)}) copy-start(f32[160,128]{1,0:T(8,128)} %param.18) | copy-start | bytes 245764
  7.0 0.8 copy-start
  84.3 1.4 %copy-start.1 = (f32[6,160,128]{2,1,0:T(8,128)S(1)}, f32[6,160,128]{2,1,0:T(8,128)}, u32[]{:S(2)}) copy-start(f32[6,160,128]{2,1,0:T(8,128)} %get-tuple-element.13) | copy-start | bytes 1474564

commit v2 on v1

--- a/solution.py
+++ b/solution.py
@@ -34,10 +34,10 @@
 
 def kernel(
     n, s, zs,
-    hid_ref, gain_ref, qt_ref, ht_ref, oc_ref, st_ref,
-    gbuf, new_ref, rms_ref,
-    hid, oc, inv, part, crecv, asend, arecv, bsend, brecv, zsend, zrecv, sbuf,
-    hsem, osem, c_s, c_r, a_s, a_r, b_s, b_r, z_s, z_r, s_s, s_r,
+    hid_ref, gain_ref, qt_ref, ht_ref, oc_ref, st0, st1, st2, st3, st4, st5,
+    gbuf_o, gbuf_q, new_ref, rms_ref,
+    st_ref, hid, oc, inv, part, crecv, asend, arecv, bsend, brecv, zsend, zrecv, sbuf, tbuf,
+    tsem, hsem, osem, c_s, c_r, a_s, a_r, b_s, b_r, z_s, z_r, s_s, s_r,
     gz_s, gz_r, gb_s, gb_r, ga_s, ga_r, gc_s, gc_r,
 ):
     tokens, width = hid.shape
@@ -75,14 +75,19 @@
         pltpu.make_async_copy(hid_ref.at[pl.ds(i * hrow, hrow)], hid.at[pl.ds(i * hrow, hrow)], hsem.at[i])
         for i in range(4)
     ]
-    for copy in oc_in + hid_in:
+    states = [pltpu.make_async_copy(ref, st_ref.at[i], tsem.at[i]) for i, ref in enumerate((st0, st1, st2, st3, st4, st5))]
+    for copy in oc_in + hid_in + states:
         copy.start()
+    gbuf = (gbuf_o, gbuf_q)
+    plane = 2 * s * s
+    spot = me % plane
 
     peer_c = dev(other, b, a, z)
     peer_a = {d: dev(core, (a + d) % s, b, z) for d in range(1, s)}
     peer_b = {d: dev(core, a, (b + d) % s, z) for d in range(1, s)}
     peer_z = {d: dev(core, a, b, (z + d) % zs) for d in range(1, zs)}
-    peers = [peer_c] + list(peer_a.values()) + list(peer_b.values()) + list(peer_z.values())
+    peer_p = {d: z * plane + (spot + d) % plane for d in range(1, plane)}
+    peers = list(peer_p.values()) + list(peer_z.values())
     barrier = pltpu.get_barrier_semaphore()
     for peer in peers:
         pl.semaphore_signal(barrier, inc=1, device_id=(peer,), device_id_type=MESH)
@@ -149,14 +154,14 @@
     def stage_b(h):
         for f in f_order:
             for e in range(1, s):
-                bsend[h, (e - 1) * zs + f] = after_a(h, e, f).astype(BF16)
+                bsend[h, (e - 1) * zs + f] = after_a(h, e, f)
                 go(copy_b(h, e, f))
 
     def after_b(h, f):
         total = after_a(h, 0, f)
         for e in range(1, s):
             copy_b(h, e, f).wait_recv()
-            total += brecv[h, (e - 1) * zs + f].astype(F32)
+            total += brecv[h, (e - 1) * zs + f]
         return total
 
     def stage_z(h):
@@ -176,7 +181,7 @@
         for k in range(per):
             part[h, i * per + k] = turned[k * rows : (k + 1) * rows]
 
-    head = ht_ref[...]
+    head = ht_ref[...].T
     for i in range(steps):
         oc_in[i].wait()
         store(0, i, jnp.dot(head, oc[:, i * chunk : (i + 1) * chunk], preferred_element_type=F32))
@@ -215,88 +220,95 @@
     part[1, me] = grad_q
 
     square = jnp.sum(grad_q * grad_q) + jnp.sum(grad_o * grad_o)
-    value = jnp.full(sbuf.shape[2:], square, F32)
+    value = jnp.full(sbuf.shape[1:], square, F32)
     at_sem = 0
-    for stage, (place, size, to) in enumerate(
-        ((core, 2, {1: peer_c}), (a, s, peer_a), (b, s, peer_b), (z, zs, peer_z))
-    ):
-        sbuf[stage, place] = value
+    for buf, place, size, to in ((sbuf, spot, plane, peer_p), (tbuf, z, zs, peer_z)):
+        buf[place] = value
         copies = []
         for d in range(1, size):
-            copy = remote(sbuf.at[stage, place], sbuf.at[stage, place], s_s.at[at_sem], s_r.at[at_sem], to[d])
+            copy = remote(buf.at[place], buf.at[place], s_s.at[at_sem], s_r.at[at_sem], to[d])
             at_sem += 1
             go(copy)
-            copies.append((d, copy))
-        for d, copy in copies:
+            copies.append(copy)
+        for copy in copies:
             copy.wait_recv()
-        value = sbuf[stage, 0]
+        value = buf[0]
         for k in range(1, size):
-            value = value + sbuf[stage, k]
+            value = value + buf[k]
     rms = jnp.sqrt(value / (2.0 * width * cols))
     rms_ref[...] = rms
     factor = jnp.minimum(1.0, clip_rms / rms)[:1]
 
-    for h in (1, 0):
+    def shard(h, d, e, f):
+        return gbuf[h].at[dev(core, (a - d + s) % s, (b - e + s) % s, (z - f + zs) % zs)]
+
+    def gather_z(h, f):
+        return remote(shard(h, 0, 0, 0), shard(h, 0, 0, 0), gz_s.at[h, f - 1], gz_r.at[h, f - 1], peer_z[f])
+
+    def gather_b(h, e, f):
+        at = (e - 1) * zs + f
+        return remote(shard(h, 0, 0, f), shard(h, 0, 0, f), gb_s.at[h, at], gb_r.at[h, at], peer_b[e])
+
+    def gather_a(h, d, e, f):
+        at = ((d - 1) * s + e) * zs + f
+        return remote(shard(h, 0, e, f), shard(h, 0, e, f), ga_s.at[h, at], ga_r.at[h, at], peer_a[d])
+
+    def gather_c(h, d, e, f):
+        at = (d * s + e) * zs + f
+        return remote(shard(h, d, e, f), shard(h, d, e, f), gc_s.at[h, at], gc_r.at[h, at], peer_c)
+
+    def pass_a(h, e, f):
+        for d in range(1, s):
+            go(gather_a(h, d, e, f))
+        go(gather_c(h, 0, e, f))
+
+    def pass_b(h, f):
+        if f:
+            gather_z(h, f).wait_recv()
+        for e in range(1, s):
+            go(gather_b(h, e, f))
+        pass_a(h, 0, f)
+
+    def from_b(h, f):
+        for e in range(1, s):
+            gather_b(h, e, f).wait_recv()
+            pass_a(h, e, f)
+
+    def from_a(h, f):
+        for e in range(s):
+            for d in range(1, s):
+                gather_a(h, d, e, f).wait_recv()
+                go(gather_c(h, d, e, f))
+
+    for copy in states:
+        copy.wait()
+    for h in range(2):
         master, moment, second = adamw(st_ref[3 * h], st_ref[3 * h + 1], st_ref[3 * h + 2], part[h, me], factor)
+        gbuf[h][me] = master.astype(BF16)
+        for f in range(1, zs):
+            go(gather_z(h, f))
+        pass_b(h, 0)
         new_ref[3 * h] = master
         new_ref[3 * h + 1] = moment
         new_ref[3 * h + 2] = second
-        gbuf[me, h] = master.astype(BF16)
-
-    def shard(d, e, f):
-        return gbuf.at[dev(core, (a - d + s) % s, (b - e + s) % s, (z - f + zs) % zs)]
-
-    def gather_z(f):
-        return remote(shard(0, 0, 0), shard(0, 0, 0), gz_s.at[f - 1], gz_r.at[f - 1], peer_z[f])
-
-    def gather_b(e, f):
-        at = (e - 1) * zs + f
-        return remote(shard(0, 0, f), shard(0, 0, f), gb_s.at[at], gb_r.at[at], peer_b[e])
-
-    def gather_a(d, e, f):
-        at = ((d - 1) * s + e) * zs + f
-        return remote(shard(0, e, f), shard(0, e, f), ga_s.at[at], ga_r.at[at], peer_a[d])
-
-    def gather_c(d, e, f):
-        at = (d * s + e) * zs + f
-        return remote(shard(d, e, f), shard(d, e, f), gc_s.at[at], gc_r.at[at], peer_c)
-
-    def pass_a(e, f):
-        for d in range(1, s):
-            go(gather_a(d, e, f))
-        go(gather_c(0, e, f))
-
-    def pass_b(f):
-        if f:
-            gather_z(f).wait_recv()
-        for e in range(1, s):
-            go(gather_b(e, f))
-        pass_a(0, f)
-
-    def from_b(f):
-        for e in range(1, s):
-            gather_b(e, f).wait_recv()
-            pass_a(e, f)
-
-    def from_a(f):
-        for e in range(s):
-            for d in range(1, s):
-                gather_a(d, e, f).wait_recv()
-                go(gather_c(d, e, f))
-
-    for f in range(1, zs):
-        go(gather_z(f))
+
     order = [0] + [f for f in (1, 3, 2) if f < zs]
     for t, f in enumerate(order):
-        pass_b(f)
-        from_b(f)
-        if t:
-            from_a(order[t - 1])
-    from_a(order[-1])
-    for d in range(s):
-        for e in range(s):
-            for f in range(zs):
-                gather_c(d, e, f).wait_recv()
+        for h in range(2):
+            if f:
+                pass_b(h, f)
+        for h in range(2):
+            from_b(h, f)
+        for h in range(2):
+            if t:
+                from_a(h, order[t - 1])
+    for h in range(2):
+        from_a(h, order[-1])
+    for h in range(2):
+        for d in range(s):
+            for e in range(s):
+                for f in range(zs):
+                    gather_c(h, d, e, f).wait_recv()
     for copy in sends:
         copy.wait_send()
 
@@ -311,22 +323,24 @@
     zs = 4
     s = math.isqrt(n // (2 * zs))
     slots = s * s * zs
-    state = jnp.stack([master_o.T, moment_o.T, second_o.T, master_q, moment_q, second_q])
+    state = (master_o.T, moment_o.T, second_o.T, master_q, moment_q, second_q)
     any_spec = pl.BlockSpec(memory_space=pl.ANY)
     vmem = pl.BlockSpec(memory_space=pltpu.VMEM)
     dma = pltpu.SemaphoreType.DMA
     na, nb, nz = (s - 1) * s * zs, (s - 1) * zs, zs - 1
     tile = (rows, cols)
-    gathered, new, rms = pl.pallas_call(
+    gathered_o, gathered_q, new, rms = pl.pallas_call(
         functools.partial(kernel, n, s, zs),
         out_shape=(
-            jax.ShapeDtypeStruct((n, 2) + tile, BF16),
+            jax.ShapeDtypeStruct((n,) + tile, BF16),
+            jax.ShapeDtypeStruct((n,) + tile, BF16),
             jax.ShapeDtypeStruct((6,) + tile, F32),
             jax.ShapeDtypeStruct((8, 128), F32),
         ),
-        in_specs=[any_spec, vmem, vmem, vmem, any_spec, vmem],
-        out_specs=(vmem, vmem, vmem),
+        in_specs=[any_spec, vmem, vmem, vmem, any_spec] + [any_spec] * 6,
+        out_specs=(vmem, vmem, vmem, vmem),
         scratch_shapes=[
+            pltpu.VMEM((6,) + tile, F32),
             pltpu.VMEM((tokens, width), BF16),
             pltpu.VMEM((tokens, width), BF16),
             pltpu.VMEM((tokens, 1), F32),
@@ -334,28 +348,29 @@
             pltpu.VMEM((2, slots) + tile, F32),
             pltpu.VMEM((2, na) + tile, BF16),
             pltpu.VMEM((2, na) + tile, BF16),
-            pltpu.VMEM((2, nb) + tile, BF16),
-            pltpu.VMEM((2, nb) + tile, BF16),
+            pltpu.VMEM((2, nb) + tile, F32),
+            pltpu.VMEM((2, nb) + tile, F32),
             pltpu.VMEM((2, nz) + tile, BF16),
             pltpu.VMEM((2, nz) + tile, BF16),
-            pltpu.VMEM((4, max(s, zs), 8, 128), F32),
-            dma((4,)), dma((64,)),
+            pltpu.VMEM((2 * s * s, 8, 128), F32),
+            pltpu.VMEM((zs, 8, 128), F32),
+            dma((6,)), dma((4,)), dma((64,)),
             dma((2, slots)), dma((2, slots)),
             dma((2, na)), dma((2, na)),
             dma((2, nb)), dma((2, nb)),
             dma((2, nz)), dma((2, nz)),
-            dma((2 * s + zs,)), dma((2 * s + zs,)),
-            dma((nz,)), dma((nz,)),
-            dma((nb,)), dma((nb,)),
-            dma((na,)), dma((na,)),
-            dma((slots,)), dma((slots,)),
+            dma((2 * s * s + zs,)), dma((2 * s * s + zs,)),
+            dma((2, nz)), dma((2, nz)),
+            dma((2, nb)), dma((2, nb)),
+            dma((2, na)), dma((2, na)),
+            dma((2, slots)), dma((2, slots)),
         ],
         compiler_params=pltpu.CompilerParams(
             collective_id=0, has_side_effects=True, vmem_limit_bytes=60 * 1024 * 1024
         ),
-    )(hidden, norm_gain[None, :], q_cotangent, head_output.T, out_cotangent, state)
-    q_param = gathered[:, 1].reshape(width, cols)
-    o_param = gathered[:, 0].reshape(width, cols).T
+    )(hidden, norm_gain[None, :], q_cotangent, head_output, out_cotangent, *state)
+    q_param = gathered_q.reshape(width, cols)
+    o_param = gathered_o.reshape(width, cols).T
     return (
         q_param, o_param,
         new[3], new[4], new[5],

time: 87 us -> 80.9 us (0.930)
  local copies, waits for them, and re-layouts: 13.4 us -> 5.59 us
  Pallas kernels: 72.4 us -> 74.4 us
    unnamed x12 -> x5, local copies, waits for them, and re-layouts: 7.07 us -> 1.06 us
    slice x1 -> x0, local copies, waits for them, and re-layouts: 2.94 us -> none  [shards(): o_param = gathered[:, 0].reshape(width, cols).T]
    reshape x0 -> x1, local copies, waits for them, and re-layouts: none -> 2.55 us  [shards(): o_param = gathered_o.reshape(width, cols).T]
    pallas_call x1, Pallas kernels: 72.4 us -> 74.4 us  [shards(): pl.pallas_call(functools.partial(kernel, n, s, zs), out_shape=(jax.ShapeD...]
    another operation x2 -> x0, local copies, waits for them, and re-layouts: 1.44 us -> none  [the longest x1 1.43 us: shards(): o_param = gathered[:, 0].reshape(width, cols).T]
where the time goes in v2:
time: 80.9 us; the launch traced here: 80.7 us
  Pallas kernels  74.4 us (92%)
  local copies, waits for them, and re-layouts  5.59 us (7%)
    pallas_call x1, Pallas kernels, shards(): pl.pallas_call(functools.partial(kernel, n, s, zs), out_shape=(jax.ShapeD...  74.4 us
    reshape x1, local copies, waits for them, and re-layouts, shards(): o_param = gathered_o.reshape(width, cols).T  2.55 us

profile of v2, /device:TPU:1, one launch (start us, length us, event | category | flops | bytes accessed | tf_op | source)
XLA Modules:
  0.0 80.7 jit_solution(4717313871167302650)
XLA Ops:
  0.6 74.4 %shard_map.178 = (bf16[32,160,128]{2,1,0:T(8,128)(2,1)}, bf16[32,160,128]{2,1,0:T(8,128)(2,1)}, f32[6,160,128]{2,1,0:T(8,128)}, f32[8,128]{1,0:T(8,128)}) custom-call(bf16[1024,5120]{1,0:T(8,128)(2,1)} %hid_ref.1, f32[1,5120]{1,0:T(1,128)} %bitcast.32, bf16[1024,128]{1,0:T(8,128)(2,1)} %qt_ref.1, bf16[1024,128]{1,0:T(8,128)(2,1)} %ht_ref.1, ...), custom_call_target="tpu_custom_call" | custom-call | tf_op jit(solution)/shard_map/pallas_call | solution.py:332
  75.1 1.2 %slice.27 = f32[1,1]{1,0:T(1,128)} slice(f32[8,128]{1,0:T(8,128)} %get-tuple-element.16), slice={[0:1], [0:1]} | slice | bytes 8 | tf_op jit(solution)/shard_map/slice | solution.py:378
  76.3 0.0 copy-start.1
  76.3 0.0 copy-start
  76.3 2.6 %copy.20 = bf16[5120,128]{0,1:T(8,128)(2,1)} copy(bf16[5120,128]{1,0:T(8,128)(2,1)} %bitcast.28) | data formatting | bytes 2621440 | tf_op jit(solution)/shard_map/reshape | solution.py:373
  78.8 0.0 copy-done.1
  78.8 0.8 slice_bitcast_fusion
  79.6 0.0 copy-done
  79.6 1.1 %copy.22 = bf16[5120,128]{1,0:T(8,128)(2,1)} copy(bf16[5120,128]{1,0:T(8,128)(2,1)S(1)} %bitcast.27) | data formatting | bytes 2621440
Async XLA Ops:
  76.3 2.6 %copy-start.1 = (f32[6,160,128]{2,1,0:T(8,128)S(1)}, f32[6,160,128]{2,1,0:T(8,128)}, u32[]{:S(2)}) copy-start(f32[6,160,128]{2,1,0:T(8,128)} %get-tuple-element.15) | copy-start | bytes 1474564
  76.3 3.3 %copy-start = (bf16[32,160,128]{2,1,0:T(8,128)(2,1)S(1)}, bf16[32,160,128]{2,1,0:T(8,128)(2,1)}, u32[]{:S(2)}) copy-start(bf16[32,160,128]{2,1,0:T(8,128)(2,1)} %get-tuple-element.13) | copy-start | bytes 3932164
